TPU v7x, 32 devices: a whole 2x2x4 slice. The times are simulated.
32 devices in a mesh: cuts: 8 (over z, y), batch: 4 (over x, core).
Axes of the slice: x: 2, y: 2, z: 4, core: 2. Of those that a mesh axis runs over, the one named last changes fastest.
Arguments:
- blocks: bfloat16 [256, 64, 128], P(('cuts', 'batch')), may hold values from -6 to 6
- environments: bfloat16 [256, 64, 128], P(('cuts', 'batch')), may hold values from -0.5 to 0.5
- layers: bfloat16 [8, 64, 128], replicated, may hold values from -0.5 to 0.5
- selectors: bfloat16 [256, 8, 128], P(('cuts', 'batch')), may hold values from -6 to 6
- classes: int32 [32, 8], P(('cuts', 'batch')), may hold values from 1 to 8
- routing: int32 [32, 8], P(('cuts', 'batch')), may hold values from 0 to 7, each once within a row
- left_edges: bfloat16 [64, 128], replicated, may hold values from -0.5 to 0.5
- right_edges: bfloat16 [64, 128], replicated, may hold values from -0.5 to 0.5
- owner_map: int32 [4096], replicated, may hold values from 0 to 4095, each once
Outputs:
- amplitudes: float32 [2, 4096], P(None, ('cuts', 'batch'))
Inputs may be any that keep to these rules, and one draw needn't show every extreme that they name: `routing`: each holder's row is a permutation of 0 to 7. `owner_map`: A permutation of the bitstrings.
All inputs are finite; a program needn't handle non-finite values.
Results may differ from a plain program's by a relative error of at most 0.009.
Values may be sent and summed in bfloat16 or wider, within the bound.
A program may use at most 64 MiB of HBM per device.

v0:
```python
import jax
import jax.numpy as jnp
from jax import lax
from jax.sharding import PartitionSpec as P


def block_form(matrix):
    half_count = matrix.shape[-1] // 2
    real_block = matrix[..., :half_count]
    imag_block = matrix[..., half_count:]
    upper_rows = jnp.concatenate([real_block, imag_block], axis=-1)
    lower_rows = jnp.concatenate([-imag_block, real_block], axis=-1)
    return jnp.concatenate([upper_rows, lower_rows], axis=-2)


def apply_phase(product, factors):
    half_count = product.shape[-1] // 2
    prod_real = product[..., :half_count]
    prod_imag = product[..., half_count:]
    fac_real = factors[..., :half_count].astype(jnp.float32)[:, None, :]
    fac_imag = factors[..., half_count:].astype(jnp.float32)[:, None, :]
    out_real = prod_real * fac_real - prod_imag * fac_imag
    out_imag = prod_real * fac_imag + prod_imag * fac_real
    return jnp.concatenate([out_real, out_imag], axis=-1)


def advance(blocks_now, factors, levels, tables):
    slot_count = blocks_now.shape[0]
    block_rows = min(32, slot_count)
    ranking = jnp.argsort(-levels, stable=True)
    blocks_now = blocks_now[ranking]
    factors = factors[ranking]
    levels = levels[ranking]
    for layer_index in range(tables.shape[0]):
        active = jnp.sum((levels > layer_index).astype(jnp.int32))
        rounds = (active + block_rows - 1) // block_rows
        layer_factors = factors[:, layer_index, :]

        def apply(round_index, current, layer_index=layer_index, layer_factors=layer_factors):
            offset = round_index * block_rows
            portion = lax.dynamic_slice_in_dim(current, offset, block_rows, 0)
            portion_levels = lax.dynamic_slice_in_dim(levels, offset, block_rows, 0)
            portion_factors = lax.dynamic_slice_in_dim(layer_factors, offset, block_rows, 0)
            product = jnp.einsum(
                "sij,jk->sik", portion, tables[layer_index], preferred_element_type=jnp.float32
            )
            updated = apply_phase(product, portion_factors).astype(jnp.bfloat16)
            portion = jnp.where((portion_levels > layer_index)[:, None, None], updated, portion)
            return lax.dynamic_update_slice_in_dim(current, portion, offset, 0)

        blocks_now = lax.fori_loop(0, rounds, apply, blocks_now)
    return (blocks_now, ranking)


def contract(worked, partners):
    slot_count, bond_width, doubled = worked.shape
    parted = worked.reshape(slot_count, bond_width, 2, bond_width)
    products = jnp.einsum("sipj,sjk->pik", parted, partners, preferred_element_type=jnp.float32)
    real_part = products[0, :, :bond_width] - products[1, :, bond_width:]
    imag_part = products[0, :, bond_width:] + products[1, :, :bond_width]
    return (real_part, imag_part)


def amplitude_table(real_part, imag_part, left_edges, right_edges, owner_map):
    highest = lax.Precision.HIGHEST
    half_count = left_edges.shape[1] // 2
    left_real = left_edges[:, :half_count].astype(jnp.float32)
    left_imag = left_edges[:, half_count:].astype(jnp.float32)
    right_real = right_edges[:, :half_count].astype(jnp.float32)
    right_imag = right_edges[:, half_count:].astype(jnp.float32)
    wave_real = jnp.dot(real_part, right_real, precision=highest) - jnp.dot(
        imag_part, right_imag, precision=highest
    )
    wave_imag = jnp.dot(real_part, right_imag, precision=highest) + jnp.dot(
        imag_part, right_real, precision=highest
    )
    amp_real = jnp.dot(left_real.T, wave_real, precision=highest) - jnp.dot(
        left_imag.T, wave_imag, precision=highest
    )
    amp_imag = jnp.dot(left_real.T, wave_imag, precision=highest) + jnp.dot(
        left_imag.T, wave_real, precision=highest
    )
    flattened = jnp.stack([amp_real.reshape(-1), amp_imag.reshape(-1)])
    return flattened[:, owner_map]


def on_device(
    blocks, environments, layers, selectors, classes, routing, left_edges, right_edges, owner_map
):
    slot_count, bond_width, doubled = blocks.shape
    cut_count = lax.axis_size("cuts")
    member = slot_count // cut_count
    tables = block_form(layers)
    levels = classes[0]
    sending = routing[0]
    worked, ranking = advance(blocks, selectors, levels, tables)
    inverse = jnp.argsort(ranking)
    outgoing = worked[inverse[sending]].reshape(cut_count, member, bond_width, doubled)
    worked = lax.all_to_all(outgoing, "cuts", split_axis=0, concat_axis=0, tiled=True).reshape(
        slot_count, bond_width, doubled
    )
    real_part, imag_part = contract(worked, environments)
    holder_count = cut_count * lax.axis_size("batch")
    normalizer = (slot_count * holder_count) ** (-0.5)
    real_part, imag_part = lax.psum((real_part, imag_part), ("cuts", "batch"))
    amp_table = (
        amplitude_table(real_part, imag_part, left_edges, right_edges, owner_map) * normalizer
    )
    per_holder = amp_table.shape[1] // holder_count
    holder = lax.axis_index("cuts") * lax.axis_size("batch") + lax.axis_index("batch")
    return lax.dynamic_slice_in_dim(amp_table, holder * per_holder, per_holder, 1)


def solution(mesh):
    placed = (
        P(("cuts", "batch"), None, None),
        P(("cuts", "batch"), None, None),
        P(),
        P(("cuts", "batch"), None, None),
        P(("cuts", "batch"), None),
        P(("cuts", "batch"), None),
        P(),
        P(),
        P(),
    )
    return jax.shard_map(
        on_device, mesh=mesh, in_specs=placed, out_specs=P(None, ("cuts", "batch")), check_vma=False
    )
```

profile of v0, /device:TPU:0, one launch (start us, length us, event | category | flops | bytes accessed | tf_op | source)
XLA Modules:
  0.0 92.8 jit_solution(10878997560112806243)
XLA Ops:
  0.0 0.7 bitcast_negate_fusion
  0.7 1.0 %sort.34 = (s32[8]{0:T(128)}, s32[8]{0:T(128)S(1)}) sort(s32[8]{0:T(128)S(1)} %bitcast_negate_fusion, s32[8]{0:T(128)S(1)} %iota.8), dimensions={0}, to_apply=%region_0.0 | sort | flops 24 | bytes 128 | tf_op jit(solution)/shard_map/jit(argsort)/sort | solution.py:30
  1.7 1.3 %gather_fusion.1 = s32[8]{0:T(128)S(1)} fusion(s32[8]{0:T(128)} %bitcast.127, s32[1024]{0:T(1024)S(1)} %pad_clamp_fusion.2), kind=kCustom, calls=%fused_computation.1 | custom fusion | bytes 96 | tf_op jit(solution)/shard_map/gather | solution.py:33
  3.0 0.8 fusion.51
  8.8 1.3 %gather_fusion.2 = bf16[8,8,128]{2,1,0:T(8,128)(2,1)S(1)} fusion(bf16[8,8,128]{2,1,0:T(8,128)(2,1)} %param.28, s32[1024]{0:T(1024)S(1)} %pad_clamp_fusion.2), kind=kCustom, calls=%fused_computation.2 | custom fusion | bytes 32800 | tf_op jit(solution)/shard_map/gather | solution.py:32
  10.1 1.1 %slice_negate_fusion = (bf16[8,64,64]{2,1,0:T(8,128)(2,1)S(1)}, bf16[8,64,64]{2,1,0:T(8,128)(2,1)S(1)}) fusion(bf16[8,64,128]{2,1,0:T(8,128)(2,1)} %param.27), kind=kLoop, calls=%fused_computation.88 | loop fusion | flops 32768 | bytes 262144 | tf_op jit(solution)/shard_map/neg | solution.py:12
  11.8 1.0 %maximum_maximum_fusion = bf16[8,128,128]{2,1,0:T(8,128)(2,1)S(1)} fusion(bf16[8,64,64]{2,1,0:T(8,128)(2,1)S(1)} %get-tuple-element.420, bf16[8,64,64]{2,1,0:T(8,128)(2,1)S(1)} %get-tuple-element.419, bf16[8,64,128]{2,1,0:T(8,128)(2,1)} %param.27), kind=kLoop, calls=%fused_computation.85 | loop fusion | flops 786432 | bytes 524288 | tf_op jit(solution)/shard_map/concatenate | solution.py:13
  12.8 0.6 while.80
  13.5 0.6 while.81
  14.1 0.6 while.82
  14.7 0.6 while.83
  15.3 0.6 while.84
  16.6 0.6 while.86
  17.3 0.6 while.87
  17.9 1.0 %sort.35 = (s32[8]{0:T(128)}, s32[8]{0:T(128)S(1)}) sort(s32[8]{0:T(128)S(1)} %get-tuple-element.271, s32[8]{0:T(128)S(1)} %iota.9), dimensions={0}, to_apply=%region_25.26 | sort | flops 24 | bytes 128 | tf_op jit(solution)/shard_map/jit(argsort)/sort | solution.py:97
  18.9 0.6 gather_fusion.3
  19.5 1.2 %gather_fusion.4 = bf16[8,64,128]{2,1,0:T(8,128)(2,1)} fusion(bf16[8,64,128]{2,1,0:T(8,128)(2,1)S(1)} %get-tuple-element.279, s32[1024]{0:T(1024)S(1)} %pad_clamp_fusion), kind=kCustom, calls=%fused_computation.4 | custom fusion | bytes 262176 | tf_op jit(solution)/shard_map/gather | solution.py:98
  20.7 7.3 %all-to-all-start = ((bf16[8,1,64,128]{3,2,1,0:T(8,128)(2,1)}), bf16[8,1,64,128]{3,2,1,0:T(8,128)(2,1)S(1)}, u32[]{:S(2)}, u32[]{:S(2)}) async-start(bf16[8,1,64,128]{3,2,1,0:T(8,128)(2,1)} %bitcast.21), calls=%async_computation | async-start | bytes 262144 | tf_op jit(solution)/shard_map/all_to_all | solution.py:99
  28.1 7.3 %all-to-all-done = bf16[8,1,64,128]{3,2,1,0:T(8,128)(2,1)S(1)} async-done(((bf16[8,1,64,128]{3,2,1,0:T(8,128)(2,1)}), bf16[8,1,64,128]{3,2,1,0:T(8,128)(2,1)S(1)}, u32[]{:S(2)}, u32[]{:S(2)}) %all-to-all-start) | async-done | bytes 131104 | tf_op jit(solution)/shard_map/all_to_all | solution.py:99
  35.9 38.6 %all-reduce = (f32[64,64]{1,0:T(8,128)S(1)}, f32[64,64]{1,0:T(8,128)S(1)}) all-reduce(f32[64,64]{1,0:T(8,128)S(1)} %get-tuple-element.422, f32[64,64]{1,0:T(8,128)S(1)} %get-tuple-element.421), channel_id=1, replica_groups=mesh['cuts'=8,'batch'=4] {'cuts','batch'}, use_global_device_ids=true, to_apply=%region_26.27 | all-reduce | flops 8192 | bytes 65536 | tf_op jit(solution)/shard_map/psum | solution.py:105
  76.5 0.6 copy.26
  77.2 14.1 %gather_fusion.5 = f32[4096,2]{1,0:T(8,128)} fusion(f32[2,4096]{0,1:T(8,128)S(1)} %copy.26, s32[4096]{0:T(1024)S(1)} %fusion.31), kind=kCustom, calls=%fused_computation.5 | custom fusion | bytes 81920 | tf_op jit(solution)/shard_map/gather | solution.py:84
  91.3 0.8 fusion.28
  92.1 0.6 copy.27
  (84 shorter events, 8.1 us)
Async XLA Ops:
  0.0 11.2 %copy-start = (bf16[8,64,128]{2,1,0:T(8,128)(2,1)S(1)}, bf16[8,64,128]{2,1,0:T(8,128)(2,1)}, u32[]{:S(2)}) copy-start(bf16[8,64,128]{2,1,0:T(8,128)(2,1)} %param.25) | copy-start | bytes 393220
  17.2 1.6 %copy-start.5 = (s32[1,8]{1,0:T(1,128)S(1)}, s32[1,8]{1,0:T(1,128)}, u32[]{:S(2)}) copy-start(s32[1,8]{1,0:T(1,128)} %param.30) | copy-start | bytes 100
  17.2 10.8 %copy-start.3 = (s32[4096]{0:T(1024)S(1)}, s32[4096]{0:T(1024)}, u32[]{:S(2)}) copy-start(s32[4096]{0:T(1024)} %param.33) | copy-start | bytes 49156
  17.2 18.3 %copy-start.4 = (bf16[8,64,128]{2,1,0:T(8,128)(2,1)S(1)}, bf16[8,64,128]{2,1,0:T(8,128)(2,1)}, u32[]{:S(2)}) copy-start(bf16[8,64,128]{2,1,0:T(8,128)(2,1)} %param.26) | copy-start | bytes 393220
  17.9 56.6 %copy-start.1 = (bf16[64,128]{1,0:T(8,128)(2,1)S(1)}, bf16[64,128]{1,0:T(8,128)(2,1)}, u32[]{:S(2)}) copy-start(bf16[64,128]{1,0:T(8,128)(2,1)} %param.32) | copy-start | bytes 49156
  17.9 57.3 %copy-start.2 = (bf16[64,128]{1,0:T(8,128)(2,1)S(1)}, bf16[64,128]{1,0:T(8,128)(2,1)}, u32[]{:S(2)}) copy-start(bf16[64,128]{1,0:T(8,128)(2,1)} %param.31) | copy-start | bytes 49156
  20.7 14.7 %all-to-all-start = ((bf16[8,1,64,128]{3,2,1,0:T(8,128)(2,1)}), bf16[8,1,64,128]{3,2,1,0:T(8,128)(2,1)S(1)}, u32[]{:S(2)}, u32[]{:S(2)}) async-start(bf16[8,1,64,128]{3,2,1,0:T(8,128)(2,1)} %bitcast.21), calls=%async_computation | async-start | bytes 262144 | tf_op jit(solution)/shard_map/all_to_all | solution.py:99
where the time goes:
time: 93.1 us; the launch traced here: 92.8 us
  blocking collectives  38.6 us (41%)
  local copies, waits for them, and re-layouts  20.9 us (22%)
  other arithmetic  9.54 us (10%)
  waiting for transfers between devices  7.32 us (8%)
  starting transfers between devices  7.31 us (8%)
  between operations  5.54 us (6%)
  matrix products  3.16 us (3%)
    psum x1, blocking collectives, on_device(): real_part, imag_part = lax.psum((real_part, imag_part), ('cuts', 'batch'))  38.6 us
    gather x1, local copies, waits for them, and re-layouts, amplitude_table(): return flattened[:, owner_map]  14.1 us
    all_to_all x1, waiting for transfers between devices, on_device(): lax.all_to_all(outgoing, 'cuts', split_axis=0, concat_axis=0, tiled=True)  7.32 us
    all_to_all x1, starting transfers between devices, on_device(): lax.all_to_all(outgoing, 'cuts', split_axis=0, concat_axis=0, tiled=True)  7.31 us
  transfers between devices with their start and end apart: 1, of which 1 were waited for; matrix products, arithmetic and copies ran while one was open for 0% of the time, Pallas kernels for 0%

commit v1 on v0

v1 whole, which is shorter than its diff:
```python
import functools

import jax
import jax.numpy as jnp
from jax import lax
from jax.experimental import pallas as pl
from jax.experimental.pallas import tpu as pltpu
from jax.sharding import PartitionSpec as P

MESH = pl.DeviceIdType.MESH
UNROLL = 32
GROUP = 8
ROWS = 4
EARLY = 2


def repeat(count, body):
    if count <= UNROLL:
        for step in range(count):
            body(step)
    else:
        lax.fori_loop(0, count, lambda step, carry: (body(step), carry)[1], 0)


def low_half(shape):
    return lax.broadcasted_iota(jnp.int32, shape, len(shape) - 1) < shape[-1] // 2


def swap(x):
    return pltpu.roll(x, x.shape[-1] // 2, x.ndim - 1)


def turn(x):
    swapped = swap(x)
    return jnp.where(low_half(x.shape), -swapped, swapped)


def split(x):
    high = x.astype(jnp.bfloat16)
    return high, (x - high.astype(jnp.float32)).astype(jnp.bfloat16)


def divide(x, by):
    if by & (by - 1) == 0:
        return lax.shift_right_logical(x, jnp.int32(by.bit_length() - 1))
    return lax.div(x, jnp.int32(by))


def kernel(
    sizes,
    blocks_hbm, env_hbm, layers_hbm, sel_hbm, cls_hbm, rout_hbm, left_hbm, right_hbm, own_hbm,
    out_ref,
    blocks, env, layers, sel, cls, rout, left, right, own,
    tables, worked, env_in, hot, left_t, right_t, send, recv,
    in_sem, env_send, env_recv, red_send, red_recv,
):
    cuts, batch = sizes
    holders = cuts * batch
    slots, bond, doubled = blocks.shape
    depth = layers.shape[0]
    member = slots // cuts
    half = doubled // 2
    chunks, unused, width = send.shape
    bits = chunks * width
    per = bits // holders
    mine, row = lax.axis_index("cuts"), lax.axis_index("batch")
    me = mine * batch + row
    f32, bf16 = jnp.float32, jnp.bfloat16

    loads = [
        pltpu.make_async_copy(src, dst, in_sem.at[i])
        for i, (src, dst) in enumerate(
            [
                (layers_hbm, layers), (blocks_hbm, blocks), (sel_hbm, sel), (cls_hbm, cls),
                (env_hbm, env), (own_hbm, own), (left_hbm, left), (right_hbm, right),
                (rout_hbm, rout),
            ]
        )
    ]
    for load in loads:
        load.start()

    barrier = pltpu.get_barrier_semaphore()

    def greet(step):
        other = lax.rem(me + step + 1, holders)
        pl.semaphore_signal(
            barrier, inc=1, device_id=(lax.div(other, batch), lax.rem(other, batch)),
            device_id_type=MESH,
        )

    repeat(holders - 1, greet)

    loads[0].wait()
    for t in range(depth):
        table = layers[t].astype(f32)
        turned = turn(table)
        tables[t, :bond, :doubled] = table.astype(bf16)
        tables[t, :bond, doubled:] = turned.astype(bf16)
        tables[t, bond:, :doubled] = turned.astype(bf16)
        tables[t, bond:, doubled:] = (-table).astype(bf16)
    for load in loads[1:4]:
        load.wait()

    def factors(base, s):
        f = sel[base + s].astype(f32)
        g = swap(f)
        low = low_half(f.shape)
        return jnp.where(low, f, g), jnp.where(low, g, f)

    def advance(base, xs, facs, start, stop):
        xs = list(xs)
        for t in range(start, stop):
            table = tables[t]
            for first in range(0, len(xs), ROWS):
                some = xs[first : first + ROWS]
                both = jnp.dot(
                    jnp.concatenate(some, axis=0), table, preferred_element_type=f32
                )
                for k, x in enumerate(some):
                    s = first + k
                    fr, fi = facs[s]
                    p = both[k * bond : (k + 1) * bond]
                    new = p[:, :doubled] * fr[t : t + 1] + p[:, doubled:] * fi[t : t + 1]
                    active = jnp.full(new.shape, cls[0, base + s], jnp.int32) > t
                    xs[s] = jnp.where(active, new, x.astype(f32)).astype(bf16)
        return xs

    group = min(GROUP, slots)
    xs = [blocks[s] for s in range(group)]
    facs = [factors(0, s) for s in range(group)]
    early = min(EARLY, depth)
    xs = advance(0, xs, facs, 0, early)

    loads[4].wait()
    pl.semaphore_wait(barrier, holders - 1)

    def env_copy(step):
        target = lax.rem(mine + step + 1, cuts)
        return pltpu.make_async_remote_copy(
            src_ref=env.at[pl.ds(target * member, member)],
            dst_ref=env_in.at[step],
            send_sem=env_send.at[step],
            recv_sem=env_recv.at[step],
            device_id=(target, row),
            device_id_type=MESH,
        )

    repeat(cuts - 1, lambda step: env_copy(step).start())

    xs = advance(0, xs, facs, early, depth)
    for s in range(group):
        worked[s] = xs[s]

    def more(index, carry):
        base = index * group
        ys = [blocks[base + s] for s in range(group)]
        ys = advance(base, ys, [factors(base, s) for s in range(group)], 0, depth)
        for s in range(group):
            worked[base + s] = ys[s]
        return carry

    if slots > group:
        lax.fori_loop(1, slots // group, more, 0)

    for load in loads[5:]:
        load.wait()
    r = right[...].astype(f32)
    l = left[...].astype(f32)
    left_t[...] = jnp.concatenate([l, l], axis=0).T.astype(bf16)
    right_t[...] = jnp.concatenate([r, turn(r)], axis=0).T.astype(bf16)
    places = lax.broadcasted_iota(jnp.int32, (half, width), 0)
    for c in range(chunks):
        high = divide(own[c : c + 1, :], half)
        ones = jnp.where(places == high, 1.0, 0.0).astype(bf16)
        hot[:half, c * width : (c + 1) * width] = ones
        hot[half:, c * width : (c + 1) * width] = ones

    zeros = jnp.zeros((bond, doubled), bf16)

    def pair(position, e):
        w = worked[rout[0, position]]
        wide = jnp.concatenate(
            [jnp.concatenate([e, zeros], axis=1), jnp.concatenate([zeros, e], axis=1)], axis=0
        )
        return jnp.dot(w, wide, preferred_element_type=f32)

    acc = jnp.zeros((bond, 2 * doubled), f32)
    for m in range(member):
        acc += pair(mine * member + m, env[mine * member + m])

    def arrive(step, acc):
        env_copy(step).wait_recv()
        source = lax.rem(mine + cuts - step - 1, cuts)
        for m in range(member):
            acc += pair(source * member + m, env_in[step, m])
        return acc

    if cuts - 1 <= UNROLL:
        for step in range(cuts - 1):
            acc = arrive(step, acc)
    else:
        acc = lax.fori_loop(0, cuts - 1, arrive, acc)
    core = acc[:, :doubled] + turn(acc[:, doubled:])

    x = jnp.dot(left_t[...], jnp.concatenate(split(core), axis=0), preferred_element_type=f32)
    v = x[:half] + turn(x[half:])
    y = lax.dot_general(
        right_t[...], jnp.concatenate(split(v), axis=0), (((1,), (1,)), ((), ())),
        preferred_element_type=f32,
    )
    y = y + swap(y)
    high, low = split(y)
    picks = jnp.where(low_half(y.shape), high.astype(f32), low.astype(f32)).astype(bf16)
    for c in range(chunks):
        z = jnp.dot(picks, hot[:, c * width : (c + 1) * width], preferred_element_type=f32)
        place = own[c : c + 1, :]
        mask = places == (place - divide(place, half) * half)
        send[c, 0:1, :] = jnp.sum(jnp.where(mask, z[:half], 0.0), axis=0, keepdims=True)
        send[c, 1:2, :] = jnp.sum(jnp.where(mask, z[half:], 0.0), axis=0, keepdims=True)

    def red_copy(step):
        other = lax.rem(me + step + 1, holders)
        return pltpu.make_async_remote_copy(
            src_ref=send.at[lax.div(other * per, width)],
            dst_ref=recv.at[step],
            send_sem=red_send,
            recv_sem=red_recv,
            device_id=(lax.div(other, batch), lax.rem(other, batch)),
            device_id_type=MESH,
        )

    repeat(holders - 1, lambda step: red_copy(step).start())
    repeat(cuts - 1, lambda step: env_copy(step).wait_send())
    total = send[lax.div(me * per, width)]
    pltpu.make_async_copy(recv, recv, red_recv).wait()
    total = total + jnp.sum(recv[...], axis=0)
    out_ref[...] = total * ((slots * holders) ** (-0.5))
    pltpu.make_async_copy(recv, recv, red_send).wait()


def on_device(sizes, blocks, environments, layers, selectors, classes, routing, left, right, own):
    cuts, batch = sizes
    holders = cuts * batch
    slots, bond, doubled = blocks.shape
    depth = layers.shape[0]
    half = left.shape[1] // 2
    bits = own.shape[0]
    per = bits // holders
    width = max(per, 128)
    chunks = bits // width
    args = (
        blocks, environments, layers, selectors, classes, routing, left, right,
        own.reshape(chunks, width),
    )
    smem = (4, 5)
    out = pl.pallas_call(
        functools.partial(kernel, sizes),
        out_shape=jax.ShapeDtypeStruct((2, width), jnp.float32),
        in_specs=[pl.BlockSpec(memory_space=pl.ANY)] * len(args),
        out_specs=pl.BlockSpec(memory_space=pltpu.VMEM),
        scratch_shapes=[
            (pltpu.SMEM if i in smem else pltpu.VMEM)(a.shape, a.dtype)
            for i, a in enumerate(args)
        ]
        + [
            pltpu.VMEM((depth, 2 * bond, 2 * doubled), jnp.bfloat16),
            pltpu.VMEM((slots, bond, doubled), jnp.bfloat16),
            pltpu.VMEM((cuts - 1, slots // cuts, bond, doubled), jnp.bfloat16),
            pltpu.VMEM((2 * half, bits), jnp.bfloat16),
            pltpu.VMEM((2 * half, 2 * bond), jnp.bfloat16),
            pltpu.VMEM((2 * half, 2 * bond), jnp.bfloat16),
            pltpu.VMEM((chunks, 2, width), jnp.float32),
            pltpu.VMEM((holders - 1, 2, width), jnp.float32),
            pltpu.SemaphoreType.DMA((len(args),)),
            pltpu.SemaphoreType.DMA((cuts - 1,)),
            pltpu.SemaphoreType.DMA((cuts - 1,)),
            pltpu.SemaphoreType.DMA,
            pltpu.SemaphoreType.DMA,
        ],
        compiler_params=pltpu.CompilerParams(collective_id=0, has_side_effects=True),
    )(*args)
    if per < width:
        holder = lax.axis_index("cuts") * batch + lax.axis_index("batch")
        out = lax.dynamic_slice_in_dim(out, lax.rem(holder * per, width), per, 1)
    return out


def solution(mesh):
    placed = (
        P(("cuts", "batch"), None, None),
        P(("cuts", "batch"), None, None),
        P(),
        P(("cuts", "batch"), None, None),
        P(("cuts", "batch"), None),
        P(("cuts", "batch"), None),
        P(),
        P(),
        P(),
    )
    sizes = (mesh.shape["cuts"], mesh.shape["batch"])
    return jax.shard_map(
        functools.partial(on_device, sizes), mesh=mesh, in_specs=placed,
        out_specs=P(None, ("cuts", "batch")), check_vma=False,
    )
```

time: 93.1 us -> 19.7 us (0.21)
  blocking collectives: 38.6 us -> 0 us
  local copies, waits for them, and re-layouts: 20.9 us -> 1.24 us
  Pallas kernels: 0 us -> 18.3 us
  other arithmetic: 9.54 us -> 0 us
  waiting for transfers between devices: 7.32 us -> 0 us
  starting transfers between devices: 7.31 us -> 0 us
  between operations: 5.54 us -> 0.01 us
  matrix products: 3.16 us -> 0 us
    psum x1 -> x0, blocking collectives: 38.6 us -> none  [on_device(): real_part, imag_part = lax.psum((real_part, imag_part), ('cuts', 'batch'))]
    gather x6 -> x0, local copies, waits for them, and re-layouts: 19.1 us -> none  [the longest x1 14.1 us: amplitude_table(): return flattened[:, owner_map]]
    pallas_call x0 -> x1, Pallas kernels: none -> 18.3 us  [on_device(): pl.pallas_call(functools.partial(kernel, sizes), out_shape=jax.ShapeDtype...]
    all_to_all x1 -> x0, waiting for transfers between devices: 7.32 us -> none  [on_device(): lax.all_to_all(outgoing, 'cuts', split_axis=0, concat_axis=0, tiled=True)]
    all_to_all x1 -> x0, starting transfers between devices: 7.31 us -> none  [on_device(): lax.all_to_all(outgoing, 'cuts', split_axis=0, concat_axis=0, tiled=True)]
    dot_general x17 -> x0, matrix products: 3.16 us -> none  [the longest x8 1.31 us: apply(): jnp.einsum('sij,jk->sik', portion, tables[layer_index], preferred_element...]
    sort x2 -> x0, other arithmetic: 1.92 us -> none  [the longest x1 0.96 us: advance(): ranking = jnp.argsort(-levels, stable=True)]
    neg x2 -> x0, other arithmetic: 1.78 us -> none  [the longest x1 1.09 us: block_form(): lower_rows = jnp.concatenate([-imag_block, real_block], axis=-1)]
  transfers between devices with their start and end apart: 1 -> 0, of which waited for: 1 -> 0; matrix products, arithmetic and copies ran while one was open for 0% -> 0% of each run, Pallas kernels for 0% -> 0%
where the time goes in v1:
time: 19.7 us; the launch traced here: 19.5 us
  Pallas kernels  18.3 us (93%)
  local copies, waits for them, and re-layouts  1.24 us (6%)
    pallas_call x1, Pallas kernels, on_device(): pl.pallas_call(functools.partial(kernel, sizes), out_shape=jax.ShapeDtype...  18.3 us
    unnamed x1, local copies, waits for them, and re-layouts  1.24 us

profile of v1, /device:TPU:0, one launch (start us, length us, event | category | flops | bytes accessed | tf_op | source)
XLA Modules:
  0.0 19.5 jit_solution(4991794228615111912)
XLA Ops:
  0.0 18.3 %shard_map.91 = f32[2,128]{1,0:T(2,128)} custom-call(bf16[8,64,128]{2,1,0:T(8,128)(2,1)} %blocks_hbm.1, bf16[8,64,128]{2,1,0:T(8,128)(2,1)} %env_hbm.1, bf16[8,64,128]{2,1,0:T(8,128)(2,1)} %layers_hbm.1, bf16[8,8,128]{2,1,0:T(8,128)(2,1)} %sel_hbm.1, s32[1,8]{1,0:T(1,128)} %cls_hbm.1, s32[1,8]{1,0:T(1,128)} %rout_hbm.1, bf16[64,128]{1,0:T(8,128)(2,1)} %left_hbm.1, ...), custom_call_target="tpu_custom_call" | custom-call | tf_op jit(solution)/shard_map/pallas_call | solution.py:257
  18.3 1.2 %copy.11 = f32[2,128]{1,0:T(2,128)} copy(f32[2,128]{1,0:T(2,128)} %shard_map.91) | data formatting | bytes 2048

commit v2 on v1

--- a/solution.py
+++ b/solution.py
@@ -89,7 +89,10 @@
             device_id_type=MESH,
         )
 
-    repeat(holders - 1, greet)
+    for step in range(cuts - 1):
+        pl.semaphore_signal(barrier, inc=1, device_id=(lax.rem(mine + step + 1, cuts), row), device_id_type=MESH)
+    for step in range(batch - 1):
+        pl.semaphore_signal(barrier, inc=1, device_id=(mine, lax.rem(row + step + 1, batch)), device_id_type=MESH)
 
     loads[0].wait()
     for t in range(depth):
@@ -133,7 +136,7 @@
     xs = advance(0, xs, facs, 0, early)
 
     loads[4].wait()
-    pl.semaphore_wait(barrier, holders - 1)
+    pl.semaphore_wait(barrier, cuts + batch - 2)
 
     def env_copy(step):
         target = lax.rem(mine + step + 1, cuts)
@@ -256,7 +259,7 @@
     smem = (4, 5)
     out = pl.pallas_call(
         functools.partial(kernel, sizes),
-        out_shape=jax.ShapeDtypeStruct((2, width), jnp.float32),
+        out_shape=pltpu.VMEM((2, width), jnp.float32),
         in_specs=[pl.BlockSpec(memory_space=pl.ANY)] * len(args),
         out_specs=pl.BlockSpec(memory_space=pltpu.VMEM),
         scratch_shapes=[

time: 19.7 us -> 18.1 us (0.919)
  Pallas kernels: 18.3 us -> 17.4 us
  local copies, waits for them, and re-layouts: 1.24 us -> 0.56 us
    pallas_call x1, Pallas kernels: 18.3 us -> 17.4 us  [on_device(): pl.pallas_call(functools.partial(kernel, sizes), out_shape=pltpu.VMEM((2,...]
    unnamed x1, local copies, waits for them, and re-layouts: 1.24 us -> 0.56 us
where the time goes in v2:
time: 18.1 us; the launch traced here: 18 us
  Pallas kernels  17.4 us (96%)
  local copies, waits for them, and re-layouts  0.56 us (3%)
    pallas_call x1, Pallas kernels, on_device(): pl.pallas_call(functools.partial(kernel, sizes), out_shape=pltpu.VMEM((2,...  17.4 us
    unnamed x1, local copies, waits for them, and re-layouts  0.56 us

profile of v2, /device:TPU:0, one launch (start us, length us, event | category | flops | bytes accessed | tf_op | source)
XLA Modules:
  0.0 18.0 jit_solution(12624211773818891431)
XLA Ops:
  0.0 17.4 %shard_map.91 = f32[2,128]{1,0:T(2,128)S(1)} custom-call(bf16[8,64,128]{2,1,0:T(8,128)(2,1)} %blocks_hbm.1, bf16[8,64,128]{2,1,0:T(8,128)(2,1)} %env_hbm.1, bf16[8,64,128]{2,1,0:T(8,128)(2,1)} %layers_hbm.1, bf16[8,8,128]{2,1,0:T(8,128)(2,1)} %sel_hbm.1, s32[1,8]{1,0:T(1,128)} %cls_hbm.1, s32[1,8]{1,0:T(1,128)} %rout_hbm.1, bf16[64,128]{1,0:T(8,128)(2,1)} %left_hbm.1, ...), custom_call_target="tpu_custom_call" | custom-call | tf_op jit(solution)/shard_map/pallas_call | solution.py:260
  17.4 0.6 %copy.11 = f32[2,128]{1,0:T(2,128)} copy(f32[2,128]{1,0:T(2,128)S(1)} %shard_map.91) | data formatting | bytes 2048

commit v3 on v2

--- a/solution.py
+++ b/solution.py
@@ -51,7 +51,7 @@
     blocks_hbm, env_hbm, layers_hbm, sel_hbm, cls_hbm, rout_hbm, left_hbm, right_hbm, own_hbm,
     out_ref,
     blocks, env, layers, sel, cls, rout, left, right, own,
-    tables, worked, env_in, hot, left_t, right_t, send, recv,
+    tables, worked, folded, env_in, hot, left_t, right_t, send, recv,
     in_sem, env_send, env_recv, red_send, red_recv,
 ):
     cuts, batch = sizes
@@ -170,8 +170,16 @@
         load.wait()
     r = right[...].astype(f32)
     l = left[...].astype(f32)
-    left_t[...] = jnp.concatenate([l, l], axis=0).T.astype(bf16)
+    left_t[...] = l.T.astype(bf16)
     right_t[...] = jnp.concatenate([r, turn(r)], axis=0).T.astype(bf16)
+
+    def fold(s):
+        x = jnp.dot(left_t[...], worked[s], preferred_element_type=f32)
+        high, low = split(x[:half] + turn(x[half:]))
+        folded[s, :, :doubled] = high
+        folded[s, :, doubled:] = low
+
+    repeat(slots, fold)
     places = lax.broadcasted_iota(jnp.int32, (half, width), 0)
     for c in range(chunks):
         high = divide(own[c : c + 1, :], half)
@@ -182,13 +190,14 @@
     zeros = jnp.zeros((bond, doubled), bf16)
 
     def pair(position, e):
-        w = worked[rout[0, position]]
+        w = folded[rout[0, position]]
         wide = jnp.concatenate(
             [jnp.concatenate([e, zeros], axis=1), jnp.concatenate([zeros, e], axis=1)], axis=0
         )
-        return jnp.dot(w, wide, preferred_element_type=f32)
-
-    acc = jnp.zeros((bond, 2 * doubled), f32)
+        twice = jnp.concatenate([wide, wide], axis=0)
+        return jnp.dot(w, twice, preferred_element_type=f32)
+
+    acc = jnp.zeros((half, 2 * doubled), f32)
     for m in range(member):
         acc += pair(mine * member + m, env[mine * member + m])
 
@@ -200,14 +209,11 @@
         return acc
 
     if cuts - 1 <= UNROLL:
-        for step in range(cuts - 1):
+        for step in sorted(range(cuts - 1), key=lambda s: min(s, cuts - 2 - s)):
             acc = arrive(step, acc)
     else:
         acc = lax.fori_loop(0, cuts - 1, arrive, acc)
-    core = acc[:, :doubled] + turn(acc[:, doubled:])
-
-    x = jnp.dot(left_t[...], jnp.concatenate(split(core), axis=0), preferred_element_type=f32)
-    v = x[:half] + turn(x[half:])
+    v = acc[:, :doubled] + turn(acc[:, doubled:])
     y = lax.dot_general(
         right_t[...], jnp.concatenate(split(v), axis=0), (((1,), (1,)), ((), ())),
         preferred_element_type=f32,
@@ -269,9 +275,10 @@
         + [
             pltpu.VMEM((depth, 2 * bond, 2 * doubled), jnp.bfloat16),
             pltpu.VMEM((slots, bond, doubled), jnp.bfloat16),
+            pltpu.VMEM((slots, half, 2 * doubled), jnp.bfloat16),
             pltpu.VMEM((cuts - 1, slots // cuts, bond, doubled), jnp.bfloat16),
             pltpu.VMEM((2 * half, bits), jnp.bfloat16),
-            pltpu.VMEM((2 * half, 2 * bond), jnp.bfloat16),
+            pltpu.VMEM((2 * half, bond), jnp.bfloat16),
             pltpu.VMEM((2 * half, 2 * bond), jnp.bfloat16),
             pltpu.VMEM((chunks, 2, width), jnp.float32),
             pltpu.VMEM((holders - 1, 2, width), jnp.float32),

time: 18.1 us -> 18 us (level)
  no operation moved by 1% of the time
where the time goes in v3:
time: 18 us; the launch traced here: 17.9 us
  Pallas kernels  17.3 us (96%)
  local copies, waits for them, and re-layouts  0.56 us (3%)
    pallas_call x1, Pallas kernels, on_device(): pl.pallas_call(functools.partial(kernel, sizes), out_shape=pltpu.VMEM((2,...  17.3 us
    unnamed x1, local copies, waits for them, and re-layouts  0.56 us

profile of v3, /device:TPU:0, one launch (start us, length us, event | category | flops | bytes accessed | tf_op | source)
XLA Modules:
  0.0 17.9 jit_solution(5346897445128525498)
XLA Ops:
  0.0 17.3 %shard_map.91 = f32[2,128]{1,0:T(2,128)S(1)} custom-call(bf16[8,64,128]{2,1,0:T(8,128)(2,1)} %blocks_hbm.1, bf16[8,64,128]{2,1,0:T(8,128)(2,1)} %env_hbm.1, bf16[8,64,128]{2,1,0:T(8,128)(2,1)} %layers_hbm.1, bf16[8,8,128]{2,1,0:T(8,128)(2,1)} %sel_hbm.1, s32[1,8]{1,0:T(1,128)} %cls_hbm.1, s32[1,8]{1,0:T(1,128)} %rout_hbm.1, bf16[64,128]{1,0:T(8,128)(2,1)} %left_hbm.1, ...), custom_call_target="tpu_custom_call" | custom-call | tf_op jit(solution)/shard_map/pallas_call | solution.py:266
  17.3 0.6 %copy.11 = f32[2,128]{1,0:T(2,128)} copy(f32[2,128]{1,0:T(2,128)S(1)} %shard_map.91) | data formatting | bytes 2048
